TPU v7x, 32 devices: a whole 2x2x4 slice. The times are simulated.
32 devices in a mesh: groups: 2 (over y), seq: 4 (over z), head: 2 (over x), rep: 2 (over core).
Axes of the slice: x: 2, y: 2, z: 4, core: 2. Of those that a mesh axis runs over, the one named last changes fastest.
Arguments:
- q_latent: bfloat16 [32, 2, 128, 512], P('groups', None, 'head'), parts along dimension 0, may hold values from -40 to 40
- q_rope: bfloat16 [32, 2, 128, 64], P('groups', None, 'head'), parts along dimension 0, may hold values from -40 to 40
- cache_latent: bfloat16 [32, 512, 512], P(('groups', 'rep'), 'seq'), parts along dimension 0, may hold values from -20 to 20
- rope_keys: bfloat16 [32, 64, 512], P(('groups', 'rep'), None, 'seq'), parts along dimension 0, may hold values from -20 to 20
- lengths: int32 [32], P(('groups', 'rep')), parts along dimension 0, may hold values from 128 to 512, as said below
- slot_request: int32 [32], P(('groups', 'rep')), parts along dimension 0, may hold values from 0 to 15, as said below
- value_up: bfloat16 [128, 512, 128], P('head'), may hold values from -0.25 to 0.25
Outputs:
- values: bfloat16 [32, 2, 128, 128], P(('groups', 'rep'), None, 'head'), parts along dimension 0
There are 2 independent parts, one for each index of `groups`. A program takes and returns all parts, laid end to end along the dimension named above; an argument that names none is the same for every part. Nothing has to cross between parts.
Inputs may be any that keep to these rules, and one draw needn't show every extreme that they name: `lengths`: each slot's length lies between 128 and 512; in every part some slot holds 512. `slot_request`: a permutation of the requests 0 to 15.
All inputs are finite; a program needn't handle non-finite values.
Results may differ from a plain program's by a relative error of at most 0.0021.
Values may be sent and summed in bfloat16 or wider, within the bound.
A program may use at most 64 MiB of HBM per device.

v0:
```python
import jax
import jax.numpy as jnp
from jax import lax
from jax.sharding import PartitionSpec as P

ROPE = 64
NOPE = 128


negative_fill = -1e30


def project(partial_value, weight):
    return jnp.einsum(
        "rthd,hdv->rthv", partial_value, weight.astype(jnp.float32), precision=lax.Precision.HIGHEST
    )


def per_device(q_latent, q_rope, cache_latent, rope_keys, lengths, slot_request, value_up):
    softmax_scale = (NOPE + ROPE) ** (-0.5)
    page_len = cache_latent.shape[1]
    new_tokens = q_latent.shape[1]
    query_lat = jnp.take(q_latent, slot_request, axis=0)
    query_rot = jnp.take(q_rope, slot_request, axis=0)
    scores = jnp.einsum(
        "rthd,rpd->rthp", query_lat, cache_latent, preferred_element_type=jnp.float32
    )
    scores = scores + jnp.einsum(
        "rthe,rep->rthp", query_rot, rope_keys, preferred_element_type=jnp.float32
    )
    scores = scores * softmax_scale
    positions = lax.axis_index("seq") * page_len + jnp.arange(page_len, dtype=jnp.int32)
    limits = lengths[:, None] - new_tokens + 1 + jnp.arange(new_tokens, dtype=jnp.int32)[None, :]
    visible = (positions[None, None, :] < limits[:, :, None])[:, :, None, :]
    masked = jnp.where(visible, scores, negative_fill)
    page_max = jnp.max(masked, axis=3)
    page_exp = jnp.where(visible, jnp.exp(masked - page_max[..., None]), 0.0)
    page_den = jnp.sum(page_exp, axis=3)
    page_out = jnp.einsum(
        "rthp,rpd->rthd",
        page_exp.astype(jnp.bfloat16),
        cache_latent,
        preferred_element_type=jnp.float32,
    )
    carried = project(page_out, value_up)
    largest = lax.pmax(page_max, "seq")
    factor = jnp.exp(page_max - largest)
    denominator, summed = lax.psum((factor * page_den, factor[..., None] * carried), "seq")
    attended = summed / denominator[..., None]
    return attended.astype(jnp.bfloat16)


def solution(mesh):
    in_specs = (
        P("groups", None, "head", None),
        P("groups", None, "head", None),
        P(("groups", "rep"), "seq", None),
        P(("groups", "rep"), None, "seq"),
        P(("groups", "rep")),
        P(("groups", "rep")),
        P("head", None, None),
    )
    out_specs = P(("groups", "rep"), None, "head", None)
    return jax.shard_map(
        per_device, mesh=mesh, in_specs=in_specs, out_specs=out_specs, check_vma=False
    )
```

profile of v0, /device:TPU:0, one launch (start us, length us, event | category | flops | bytes accessed | tf_op | source)
XLA Modules:
  0.0 82.9 jit_solution(7256757817317256383)
XLA Ops:
  6.5 0.0 copy-start
  6.5 0.0 copy-start.3
  6.5 0.0 copy-start.2
  6.5 0.0 all-reduce.2.cloned.1.call-start
  6.5 0.8 compare_select_fusion
  7.4 0.7 compare_and_fusion
  8.0 1.6 %gather_fusion.1 = bf16[8,2,64,64]{3,2,1,0:T(8,128)(2,1)S(1)} fusion(bf16[16,2,64,64]{3,2,1,0:T(8,128)(2,1)} %param.8, s32[1024]{0:T(1024)S(1)} %pad_clamp_fusion), kind=kCustom, calls=%fused_computation.1 | custom fusion | bytes 262176 | tf_op jit(solution)/shard_map/jit(_take)/gather | solution.py:24
  9.7 0.0 copy-done
  9.7 0.6 gather_fusion
  10.3 0.0 copy-done.3
  10.3 0.1 iota_add_fusion
  10.4 0.1 broadcast_compare_fusion
  10.5 0.0 copy-done.2
  10.5 0.0 copy-start.1
  10.5 0.3 fusion.26
  10.8 1.8 %fusion.36 = (f32[8,2,64]{2,1,0:T(2,128)S(1)}, f32[8,2,64,128]{3,2,1,0:T(8,128)S(1)}) fusion(f32[8,2,64,128]{3,2,1,0:T(8,128)S(1)} %fusion.26, bf16[8,128,512]{2,1,0:T(8,128)(2,1)} %param.9, bf16[8,2,64,512]{3,2,1,0:T(8,128)(2,1)S(1)} %gather_fusion, pred[8]{0:T(512)(128)(4,1)S(1)} %compare_and_fusion, pred[8,2,128]{2,1,0:T(4,128)(4,1)S(1)} %broadcast_compare_fusion), kind=kOutput, calls=%fused_computation.40 | convolution fusion | flops 135265280 | bytes 3151880 | tf_op jit(solution)/shard_map/rthd,rpd->rthp/dot_general | solution.py:25
  12.6 0.0 copy-done.1
  12.6 1.8 %fusion.15 = f32[8,2,64,512]{3,2,1,0:T(8,128)} fusion(bf16[8,128,512]{2,1,0:T(8,128)(2,1)S(1)} %copy-done.1, f32[8,2,64,128]{3,2,1,0:T(8,128)S(1)} %get-tuple-element.8, f32[8,2,64]{2,1,0:T(2,128)S(1)} %get-tuple-element.7, pred[8,2,128]{2,1,0:T(4,128)(4,1)S(1)} %broadcast_compare_fusion), kind=kOutput, calls=%fused_computation.10 | convolution fusion | flops 134610944 | bytes 3676160 | tf_op jit(solution)/shard_map/rthp,rpd->rthd/dot_general | solution.py:39
  14.5 0.4 fusion.21
  14.9 13.7 %pmax.7 = f32[8,2,64]{2,1,0:T(2,128)S(1)} all-reduce(f32[8,2,64]{2,1,0:T(2,128)S(1)} %get-tuple-element.7), channel_id=1, replica_groups=mesh['groups'=2,'seq'=4,'head'=2,'rep'=2] {'seq'}, use_global_device_ids=true, to_apply=%region_1.2 | all-reduce | flops 1024 | bytes 8192 | tf_op jit(solution)/shard_map/pmax | solution.py:46
  28.6 0.1 copy.8
  28.8 8.1 %fusion.10 = f32[8,2,64,128]{3,0,1,2:T(8,128)} fusion(bf16[64,512,128]{2,1,0:T(8,128)(2,1)} %param.13, f32[8,2,64,512]{3,2,1,0:T(8,128)} %fusion.15, f32[8,2,64]{0,1,2:T(2,128)S(1)} %copy.8), kind=kOutput, calls=%fused_computation.9 | convolution fusion | flops 805437440 | bytes 11014144 | tf_op jit(solution)/shard_map/rthd,hdv->rthv/dot_general | solution.py:14
  36.9 0.0 all-reduce.2.cloned.1.call-update
  36.9 8.5 %psum.15 = f32[8,2,64]{2,1,0:T(2,128)S(1)} all-reduce(f32[8,2,64]{2,1,0:T(2,128)S(1)} %bitcast.35), channel_id=1, replica_groups=mesh['groups'=2,'seq'=4,'head'=2,'rep'=2] {'seq'}, use_global_device_ids=true, to_apply=%region_4.5 | all-reduce | flops 1024 | bytes 8192 | tf_op jit(solution)/shard_map/psum | solution.py:48
  45.5 0.1 copy.9
  45.6 28.5 %all-reduce.2.cloned.1.call-done = f32[8,2,64,128]{3,0,1,2:T(8,128)} async-done(((f32[8,2,64,128]{3,0,1,2:T(8,128)}), f32[8,2,64,128]{3,0,1,2:T(8,128)}) %all-reduce.2.cloned.1.call-update) | async-done | bytes 524304 | tf_op jit(solution)/shard_map/psum | solution.py:48
  74.0 1.2 %divide_convert_fusion = bf16[8,2,64,128]{3,0,1,2:T(8,128)(2,1)S(1)} fusion(f32[8,2,64,128]{3,0,1,2:T(8,128)} %all-reduce.2.cloned.1.call-done, f32[8,2,64]{0,1,2:T(2,128)S(1)} %copy.9), kind=kLoop, calls=%fused_computation.15 | loop fusion | flops 262144 | bytes 790528 | tf_op jit(solution)/shard_map/convert_element_type | solution.py:50
  75.3 0.8 copy.10
  (4 shorter events, 0.0 us)
Async XLA Ops:
  6.5 3.1 %copy-start = (bf16[16,2,64,512]{3,2,1,0:T(8,128)(2,1)S(1)}, bf16[16,2,64,512]{3,2,1,0:T(8,128)(2,1)}, u32[]{:S(2)}) copy-start(bf16[16,2,64,512]{3,2,1,0:T(8,128)(2,1)} %param.7) | copy-start | bytes 6291460
  6.5 3.8 %copy-start.3 = (s32[8]{0:T(128)S(1)}, s32[8]{0:T(128)}, u32[]{:S(2)}) copy-start(s32[8]{0:T(128)} %param.11) | copy-start | bytes 100
  6.5 3.9 %copy-start.2 = (bf16[8,64,128]{2,1,0:T(8,128)(2,1)S(1)}, bf16[8,64,128]{2,1,0:T(8,128)(2,1)}, u32[]{:S(2)}) copy-start(bf16[8,64,128]{2,1,0:T(8,128)(2,1)} %param.10) | copy-start | bytes 393220
  6.5 67.5 %all-reduce.2.cloned.1.call-start = ((), (), s32[]{:S(2)}) async-start(), calls=%async_computation | async-start | bytes 1048576 | tf_op jit(solution)/shard_map/psum | solution.py:48
  10.5 2.1 %copy-start.1 = (bf16[8,128,512]{2,1,0:T(8,128)(2,1)S(1)}, bf16[8,128,512]{2,1,0:T(8,128)(2,1)}, u32[]{:S(2)}) copy-start(bf16[8,128,512]{2,1,0:T(8,128)(2,1)} %param.9) | copy-start | bytes 3145732
Sparse Core Ops, SparseCore 0:
  37.0 36.9 all-reduce.1
where the time goes:
time: 83.2 us; the launch traced here: 82.9 us
  waiting for transfers between devices  28.5 us (34%)
  blocking collectives  22.3 us (27%)
  between operations  13.5 us (16%)
  matrix products  12.1 us (15%)
  other arithmetic  3.3 us (4%)
  local copies, waits for them, and re-layouts  3.26 us (4%)
    psum x1, waiting for transfers between devices, per_device(): lax.psum((factor * page_den, factor[..., None] * carried), 'seq')  28.5 us
    pmax x1, blocking collectives, per_device(): largest = lax.pmax(page_max, 'seq')  13.7 us
    psum x1, blocking collectives, per_device(): lax.psum((factor * page_den, factor[..., None] * carried), 'seq')  8.52 us
    dot_general x1, matrix products, project(): jnp.einsum('rthd,hdv->rthv', partial_value, weight.astype(jnp.float32), p...  8.14 us
    dot_general x1, matrix products, per_device(): jnp.einsum('rthp,rpd->rthd', page_exp.astype(jnp.bfloat16), cache_latent,...  1.84 us
    dot_general x1, matrix products, per_device(): jnp.einsum('rthd,rpd->rthp', query_lat, cache_latent, preferred_element_t...  1.84 us
  transfers between devices with their start and end apart: 1, of which 1 were waited for; matrix products, arithmetic and copies ran while one was open for 0% of the time, Pallas kernels for 0%

commit v1 on v0

v1 whole, which is shorter than its diff:
```python
import functools

import jax
import jax.numpy as jnp
from jax import lax
from jax.experimental import pallas as pl
from jax.experimental.pallas import tpu as pltpu
from jax.sharding import PartitionSpec as P

ROPE = 64
NOPE = 128
MESH = pl.DeviceIdType.MESH
LANES = 128


negative_fill = -1e30


def kernel(n, lengths_ref, request_ref, qlat_hbm, qrot_hbm, cache_hbm, rope_hbm, w_hbm, out_ref,
           qlat, qrot, cache, rope, w, weights, x, own, stat_out, stat_in, send, recv,
           load_sem, w_sem, stat_ssem, stat_rsem, rs_ssem, rs_rsem, ag_ssem, ag_rsem):
    slots, page, latent = cache.shape
    toks, heads = qlat.shape[1], qlat.shape[2]
    rows = toks * heads
    group = toks * slots
    per = heads // n
    me = lax.axis_index("seq")
    order = sorted(range(1, n), key=lambda k: abs(k - n / 2)) + [0]

    def peer(k):
        return lax.rem(me + k, n)

    loads = [
        pltpu.make_async_copy(src, dst, load_sem.at[i])
        for i, (src, dst) in enumerate(
            ((qlat_hbm, qlat), (cache_hbm, cache), (qrot_hbm, qrot), (rope_hbm, rope)))
    ]
    for copy in loads:
        copy.start()

    def w_load(k):
        part = pl.ds(peer(k) * per, per)
        return pltpu.make_async_copy(w_hbm.at[part], w.at[part], w_sem.at[k])

    for k in order:
        w_load(k).start()

    barrier = pltpu.get_barrier_semaphore()
    for k in range(1, n):
        pl.semaphore_signal(barrier, inc=1, device_id={"seq": peer(k)}, device_id_type=MESH)

    for copy in loads:
        copy.wait()

    softmax_scale = (NOPE + ROPE) ** (-0.5)
    lane = lax.broadcasted_iota(jnp.int32, (rows, LANES), 1)
    token = lax.broadcasted_iota(jnp.int32, (rows, page), 0) // heads
    position = me * page + lax.broadcasted_iota(jnp.int32, (rows, page), 1)
    stat = jnp.zeros((rows, LANES), jnp.float32)
    for b in range(slots):
        r = request_ref[b]
        ql = qlat[r].reshape(rows, latent)
        qr = qrot[r].reshape(rows, qrot.shape[3])
        s = lax.dot_general(ql, cache[b], (((1,), (1,)), ((), ())), preferred_element_type=jnp.float32)
        s = s + jnp.dot(qr, rope[b], preferred_element_type=jnp.float32)
        s = s * softmax_scale
        visible = position < lengths_ref[b] - toks + 1 + token
        masked = jnp.where(visible, s, negative_fill)
        top = jnp.max(masked, axis=1, keepdims=True)
        e = jnp.where(visible, jnp.exp(masked - top), 0.0)
        den = jnp.sum(e, axis=1, keepdims=True)
        stat = jnp.where(lane == b, top, stat)
        stat = jnp.where(lane == slots + b, den, stat)
        weights[b] = e.astype(jnp.bfloat16)
    width = stat_out.shape[1]
    if rows < width:
        stat = jnp.concatenate([stat, jnp.zeros((width - rows, LANES), jnp.float32)], axis=0)
    mine = jnp.transpose(stat)[: 2 * slots]
    stat_out[...] = mine

    pl.semaphore_wait(barrier, n - 1)

    def stat_copy(k):
        return pltpu.make_async_remote_copy(
            src_ref=stat_out, dst_ref=stat_in.at[k], send_sem=stat_ssem.at[k], recv_sem=stat_rsem.at[k],
            device_id={"seq": peer(k)}, device_id_type=MESH)

    def rs_copy(k):
        return pltpu.make_async_remote_copy(
            src_ref=send.at[k], dst_ref=recv.at[k], send_sem=rs_ssem.at[k], recv_sem=rs_rsem.at[k],
            device_id={"seq": peer(k)}, device_id_type=MESH)

    def ag_copy(k):
        part = out_ref.at[pl.ds(me * per, per)]
        return pltpu.make_async_remote_copy(
            src_ref=part, dst_ref=part, send_sem=ag_ssem.at[k], recv_sem=ag_rsem.at[k],
            device_id={"seq": peer(k)}, device_id_type=MESH)

    for k in order[:-1]:
        stat_copy(k).start()

    for b in range(slots):
        po = jnp.dot(weights[b], cache[b], preferred_element_type=jnp.float32)
        for t in range(toks):
            for c in range(latent // LANES):
                x[c, pl.ds(t * slots + b, heads, stride=group), :] = (
                    po[t * heads:(t + 1) * heads, c * LANES:(c + 1) * LANES])

    for k in range(1, n):
        stat_copy(k).wait_recv()
    tops = [mine[:slots]] + [stat_in[k, :slots, :] for k in range(1, n)]
    dens = [mine[slots:]] + [stat_in[k, slots:, :] for k in range(1, n)]
    largest = functools.reduce(jnp.maximum, tops)
    total = functools.reduce(lambda a, b: a + b, [jnp.exp(t - largest) * d for t, d in zip(tops, dens)])
    coef = jnp.exp(tops[0] - largest) / total
    coef = jnp.concatenate(
        [coef if t == 0 else pltpu.roll(coef, width - t * heads, 1) for t in range(toks)], axis=0)

    for k in order:
        w_load(k).wait()
        dest = peer(k)
        turned = pltpu.roll(coef, lax.rem(width - dest * per, width), 1)
        parts = []
        for j in range(per):
            h = dest * per + j
            base = pl.multiple_of(h * group, group)
            xs = jnp.concatenate([x[c, pl.ds(base, group), :] for c in range(latent // LANES)], axis=1)
            hi = xs.astype(jnp.bfloat16)
            lo = (xs - hi.astype(jnp.float32)).astype(jnp.bfloat16)
            both = jnp.dot(jnp.concatenate([hi, lo], axis=0), w[h], preferred_element_type=jnp.float32)
            parts.append((both[:group] + both[group:]) * turned[:, j:j + 1])
        if k == 0:
            for j in range(per):
                own[j] = parts[j]
        else:
            for j in range(per):
                send[k, j] = parts[j]
            rs_copy(k).start()

    for k in order[:-1]:
        rs_copy(k).wait_recv()
    for j in range(per):
        acc = own[j]
        for k in range(1, n):
            acc = acc + recv[k, j]
        out_ref[me * per + j] = acc.astype(jnp.bfloat16)
    for k in order[:-1]:
        ag_copy(k).start()
    for k in order[:-1]:
        stat_copy(k).wait_send()
        rs_copy(k).wait_send()
    for k in order[:-1]:
        ag_copy(k).wait()


def per_device(n, q_latent, q_rope, cache_latent, rope_keys, lengths, slot_request, value_up):
    toks, heads = q_latent.shape[1], q_latent.shape[2]
    slots, page, latent = cache_latent.shape
    dv = value_up.shape[2]
    group = toks * slots
    per = heads // n
    rows = toks * heads
    width = -(-rows // LANES) * LANES
    hbm = pl.BlockSpec(memory_space=pltpu.HBM)
    smem = pl.BlockSpec(memory_space=pltpu.SMEM)
    dma = pltpu.SemaphoreType.DMA
    out = pl.pallas_call(
        functools.partial(kernel, n),
        out_shape=jax.ShapeDtypeStruct((heads, group, dv), jnp.bfloat16),
        in_specs=[smem, smem, hbm, hbm, hbm, hbm, hbm],
        out_specs=pl.BlockSpec(memory_space=pltpu.VMEM),
        scratch_shapes=[
            pltpu.VMEM(q_latent.shape, jnp.bfloat16),
            pltpu.VMEM(q_rope.shape, jnp.bfloat16),
            pltpu.VMEM(cache_latent.shape, jnp.bfloat16),
            pltpu.VMEM(rope_keys.shape, jnp.bfloat16),
            pltpu.VMEM(value_up.shape, jnp.bfloat16),
            pltpu.VMEM((slots, rows, page), jnp.bfloat16),
            pltpu.VMEM((latent // LANES, heads * group, LANES), jnp.float32),
            pltpu.VMEM((per, group, dv), jnp.float32),
            pltpu.VMEM((2 * slots, width), jnp.float32),
            pltpu.VMEM((n, 2 * slots, width), jnp.float32),
            pltpu.VMEM((n, per, group, dv), jnp.float32),
            pltpu.VMEM((n, per, group, dv), jnp.float32),
            dma((4,)), dma((n,)), dma((n,)), dma((n,)), dma((n,)), dma((n,)),
            dma((n,)), dma((n,)),
        ],
        compiler_params=pltpu.CompilerParams(
            collective_id=0, has_side_effects=True, vmem_limit_bytes=67043328),
    )(lengths, slot_request, q_latent, q_rope, cache_latent, rope_keys, value_up)
    return jnp.transpose(out.reshape(heads, toks, slots, dv), (2, 1, 0, 3))


def solution(mesh):
    in_specs = (
        P("groups", None, "head", None),
        P("groups", None, "head", None),
        P(("groups", "rep"), "seq", None),
        P(("groups", "rep"), None, "seq"),
        P(("groups", "rep")),
        P(("groups", "rep")),
        P("head", None, None),
    )
    out_specs = P(("groups", "rep"), None, "head", None)
    return jax.shard_map(
        functools.partial(per_device, mesh.shape["seq"]),
        mesh=mesh, in_specs=in_specs, out_specs=out_specs, check_vma=False,
    )
```

time: 83.2 us -> 32.2 us (0.39)
  Pallas kernels: 0 us -> 30.3 us
  waiting for transfers between devices: 28.5 us -> 0 us
  blocking collectives: 22.3 us -> 0 us
  between operations: 13.5 us -> 0.01 us
  matrix products: 12.1 us -> 0 us
  other arithmetic: 3.3 us -> 0 us
  local copies, waits for them, and re-layouts: 3.26 us -> 1.72 us
    pallas_call x0 -> x1, Pallas kernels: none -> 30.3 us  [per_device(): pl.pallas_call(functools.partial(kernel, n), out_shape=jax.ShapeDtypeStru...]
    psum x1 -> x0, waiting for transfers between devices: 28.5 us -> none  [per_device(): lax.psum((factor * page_den, factor[..., None] * carried), 'seq')]
    pmax x1 -> x0, blocking collectives: 13.7 us -> none  [per_device(): largest = lax.pmax(page_max, 'seq')]
    dot_general x4 -> x0, matrix products: 12.1 us -> none  [the longest x1 8.14 us: project(): jnp.einsum('rthd,hdv->rthv', partial_value, weight.astype(jnp.float32), p...]
    psum x1 -> x0, blocking collectives: 8.52 us -> none  [per_device(): lax.psum((factor * page_den, factor[..., None] * carried), 'seq')]
    gather x2 -> x0, local copies, waits for them, and re-layouts: 2.25 us -> none  [the longest x1 1.64 us: per_device(): query_rot = jnp.take(q_rope, slot_request, axis=0)]
    reshape x0 -> x1, local copies, waits for them, and re-layouts: none -> 1.72 us  [per_device(): return jnp.transpose(out.reshape(heads, toks, slots, dv), (2, 1, 0, 3))]
    convert_element_type x1 -> x0, other arithmetic: 1.25 us -> none  [per_device(): return attended.astype(jnp.bfloat16)]
  transfers between devices with their start and end apart: 1 -> 0, of which waited for: 1 -> 0; matrix products, arithmetic and copies ran while one was open for 0% -> 0% of each run, Pallas kernels for 0% -> 0%
where the time goes in v1:
time: 32.2 us; the launch traced here: 32 us
  Pallas kernels  30.3 us (94%)
  local copies, waits for them, and re-layouts  1.72 us (5%)
    pallas_call x1, Pallas kernels, per_device(): pl.pallas_call(functools.partial(kernel, n), out_shape=jax.ShapeDtypeStru...  30.3 us
    reshape x1, local copies, waits for them, and re-layouts, per_device(): return jnp.transpose(out.reshape(heads, toks, slots, dv), (2, 1, 0, 3))  1.72 us

profile of v1, /device:TPU:0, one launch (start us, length us, event | category | flops | bytes accessed | tf_op | source)
XLA Modules:
  0.0 32.0 jit_solution(3591405556248429647)
XLA Ops:
  0.0 30.3 %shard_map.73 = bf16[64,16,128]{2,1,0:T(8,128)(2,1)} custom-call(s32[8]{0:T(128)} %lengths_ref.1, s32[8]{0:T(128)} %request_ref.1, bf16[16,2,64,512]{3,2,1,0:T(8,128)(2,1)} %qlat_hbm.1, bf16[16,2,64,64]{3,2,1,0:T(8,128)(2,1)} %qrot_hbm.1, bf16[8,128,512]{2,1,0:T(8,128)(2,1)} %cache_hbm.1, bf16[8,64,128]{2,1,0:T(8,128)(2,1)} %rope_hbm.1, ...), custom_call_target="tpu_custom_call" | custom-call | tf_op jit(solution)/shard_map/pallas_call | solution.py:167
  30.3 1.7 %copy.10 = bf16[64,2,8,128]{3,0,1,2:T(8,128)(2,1)} copy(bf16[64,2,8,128]{3,2,1,0:T(8,128)(2,1)} %bitcast.4) | data formatting | bytes 524288 | tf_op jit(solution)/shard_map/reshape | solution.py:191

commit v2 on v1

v2 whole, which is shorter than its diff:
```python
import functools

import jax
import jax.numpy as jnp
from jax import lax
from jax.experimental import pallas as pl
from jax.experimental.pallas import tpu as pltpu
from jax.sharding import PartitionSpec as P

ROPE = 64
NOPE = 128
MESH = pl.DeviceIdType.MESH
LANES = 128
CUTS = 2
CODE = 32767.0


negative_fill = -1e30


def kernel(n, cuts, lengths_ref, request_ref, qlat_hbm, qrot_hbm, cache_hbm, rope_hbm, w_hbm, out_ref,
           qlat, qrot, cache, rope, w, weights, x, own, stat_out, stat_in, send, recv, scale_out, scale_in,
           load_sem, w_sem, stat_ssem, stat_rsem, rs_ssem, rs_rsem, sc_ssem, sc_rsem, ag_ssem, ag_rsem):
    slots, page, latent = cache.shape
    toks, heads = qlat.shape[1], qlat.shape[2]
    rows = toks * heads
    group = toks * slots
    per = heads // n
    cut = per // cuts
    me = lax.axis_index("seq")
    order = sorted(range(1, n), key=lambda k: abs(k - n / 2))
    steps = [(c, k) for c in range(cuts) for k in order] + [(c, 0) for c in range(cuts)]

    def peer(k):
        return lax.rem(me + k, n)

    loads = [
        pltpu.make_async_copy(src, dst, load_sem.at[i])
        for i, (src, dst) in enumerate(
            ((qlat_hbm, qlat), (cache_hbm, cache), (qrot_hbm, qrot), (rope_hbm, rope)))
    ]
    for copy in loads:
        copy.start()

    def w_load(c, k):
        part = pl.ds(peer(k) * per + c * cut, cut)
        return pltpu.make_async_copy(w_hbm.at[part], w.at[part], w_sem.at[c, k])

    for c, k in steps:
        w_load(c, k).start()

    barrier = pltpu.get_barrier_semaphore()
    for k in order:
        pl.semaphore_signal(barrier, inc=1, device_id={"seq": peer(k)}, device_id_type=MESH)

    for copy in loads:
        copy.wait()

    softmax_scale = (NOPE + ROPE) ** (-0.5)
    lane = lax.broadcasted_iota(jnp.int32, (rows, LANES), 1)
    token = lax.broadcasted_iota(jnp.int32, (rows, page), 0) // heads
    position = me * page + lax.broadcasted_iota(jnp.int32, (rows, page), 1)
    stat = jnp.zeros((rows, LANES), jnp.float32)
    for b in range(slots):
        r = request_ref[b]
        ql = qlat[r].reshape(rows, latent)
        qr = qrot[r].reshape(rows, qrot.shape[3])
        s = lax.dot_general(ql, cache[b], (((1,), (1,)), ((), ())), preferred_element_type=jnp.float32)
        s = s + jnp.dot(qr, rope[b], preferred_element_type=jnp.float32)
        s = s * softmax_scale
        visible = position < lengths_ref[b] - toks + 1 + token
        masked = jnp.where(visible, s, negative_fill)
        top = jnp.max(masked, axis=1, keepdims=True)
        e = jnp.where(visible, jnp.exp(masked - top), 0.0)
        den = jnp.sum(e, axis=1, keepdims=True)
        stat = jnp.where(lane == b, top, stat)
        stat = jnp.where(lane == slots + b, den, stat)
        weights[b] = e.astype(jnp.bfloat16)
    width = stat_out.shape[1]
    if rows < width:
        stat = jnp.concatenate([stat, jnp.zeros((width - rows, LANES), jnp.float32)], axis=0)
    mine = jnp.transpose(stat)[: 2 * slots]
    stat_out[...] = mine

    def remote(src, dst, ssem, rsem, k):
        return pltpu.make_async_remote_copy(
            src_ref=src, dst_ref=dst, send_sem=ssem, recv_sem=rsem,
            device_id={"seq": peer(k)}, device_id_type=MESH)

    def stat_copy(k):
        return remote(stat_out, stat_in.at[k], stat_ssem.at[k], stat_rsem.at[k], k)

    def rs_copy(c, k):
        return remote(send.at[c, k], recv.at[c, k], rs_ssem.at[c, k], rs_rsem.at[c, k], k)

    def sc_copy(c, k):
        return remote(scale_out.at[c, k], scale_in.at[c, k], sc_ssem.at[c, k], sc_rsem.at[c, k], k)

    def ag_copy(c, k):
        part = out_ref.at[pl.ds(me * per + c * cut, cut)]
        return remote(part, part, ag_ssem.at[c, k], ag_rsem.at[c, k], k)

    for b in range(slots):
        po = jnp.dot(weights[b], cache[b], preferred_element_type=jnp.float32)
        for t in range(toks):
            for i in range(latent // LANES):
                x[i, pl.ds(t * slots + b, heads, stride=group), :] = (
                    po[t * heads:(t + 1) * heads, i * LANES:(i + 1) * LANES])

    scale_lane = lax.broadcasted_iota(jnp.int32, scale_out.shape[2:], 1)
    for number, (c, k) in enumerate(steps):
        w_load(c, k).wait()
        scale = jnp.zeros(scale_out.shape[2:], jnp.float32)
        for j in range(cut):
            h = peer(k) * per + c * cut + j
            base = pl.multiple_of(h * group, group)
            xs = jnp.concatenate([x[i, pl.ds(base, group), :] for i in range(latent // LANES)], axis=1)
            hi = xs.astype(jnp.bfloat16)
            lo = (xs - hi.astype(jnp.float32)).astype(jnp.bfloat16)
            both = jnp.dot(jnp.concatenate([hi, lo], axis=0), w[h], preferred_element_type=jnp.float32)
            part = both[:group] + both[group:]
            if k == 0:
                own[c * cut + j] = part
            else:
                peak = jnp.maximum(jnp.max(jnp.abs(part), axis=1, keepdims=True), 1e-30)
                send[c, k, j] = jnp.round(part * (CODE / peak)).astype(jnp.int32).astype(jnp.int16)
                for t in range(toks):
                    scale = jnp.where(scale_lane == t * cut + j, peak[t * slots:(t + 1) * slots], scale)
        if k != 0:
            scale_out[c, k] = scale * (1.0 / CODE)
            if number == 0:
                pl.semaphore_wait(barrier, n - 1)
                for other in order:
                    stat_copy(other).start()
            sc_copy(c, k).start()
            rs_copy(c, k).start()

    for k in order:
        stat_copy(k).wait_recv()
    tops = [mine[:slots]] + [stat_in[k, :slots, :] for k in range(1, n)]
    dens = [mine[slots:]] + [stat_in[k, slots:, :] for k in range(1, n)]
    largest = functools.reduce(jnp.maximum, tops)
    factors = [jnp.exp(t - largest) for t in tops]
    total = functools.reduce(lambda a, b: a + b, [f * d for f, d in zip(factors, dens)])

    for c in range(cuts):
        for k in order:
            sc_copy(c, k).wait_recv()
            rs_copy(c, k).wait_recv()
        coefs = []
        for k in range(n):
            ratio = factors[k] / total
            halves = []
            for t in range(toks):
                shift = lax.rem(2 * width - t * heads - me * per - c * cut, width)
                turned = pltpu.roll(ratio, shift, 1)
                if k:
                    scale = scale_in[c, k]
                    turned = turned * (pltpu.roll(scale, width - t * cut, 1) if t else scale)
                halves.append(turned)
            coefs.append(jnp.concatenate(halves, axis=0))
        for j in range(cut):
            acc = own[c * cut + j] * coefs[0][:, j:j + 1]
            for k in range(1, n):
                acc = acc + recv[c, k, j].astype(jnp.float32) * coefs[k][:, j:j + 1]
            out_ref[me * per + c * cut + j] = acc.astype(jnp.bfloat16)
        for k in order:
            ag_copy(c, k).start()
    for k in order:
        stat_copy(k).wait_send()
        for c in range(cuts):
            sc_copy(c, k).wait_send()
            rs_copy(c, k).wait_send()
    for c in range(cuts):
        for k in order:
            ag_copy(c, k).wait()


def per_device(n, q_latent, q_rope, cache_latent, rope_keys, lengths, slot_request, value_up):
    toks, heads = q_latent.shape[1], q_latent.shape[2]
    slots, page, latent = cache_latent.shape
    dv = value_up.shape[2]
    group = toks * slots
    per = heads // n
    cuts = CUTS if per % (4 * CUTS) == 0 else 1
    cut = per // cuts
    rows = toks * heads
    width = -(-rows // LANES) * LANES
    hbm = pl.BlockSpec(memory_space=pltpu.HBM)
    smem = pl.BlockSpec(memory_space=pltpu.SMEM)
    dma = pltpu.SemaphoreType.DMA
    out = pl.pallas_call(
        functools.partial(kernel, n, cuts),
        out_shape=jax.ShapeDtypeStruct((heads, group, dv), jnp.bfloat16),
        in_specs=[smem, smem, hbm, hbm, hbm, hbm, hbm],
        out_specs=pl.BlockSpec(memory_space=pltpu.VMEM),
        scratch_shapes=[
            pltpu.VMEM(q_latent.shape, jnp.bfloat16),
            pltpu.VMEM(q_rope.shape, jnp.bfloat16),
            pltpu.VMEM(cache_latent.shape, jnp.bfloat16),
            pltpu.VMEM(rope_keys.shape, jnp.bfloat16),
            pltpu.VMEM(value_up.shape, jnp.bfloat16),
            pltpu.VMEM((slots, rows, page), jnp.bfloat16),
            pltpu.VMEM((latent // LANES, heads * group, LANES), jnp.float32),
            pltpu.VMEM((per, group, dv), jnp.float32),
            pltpu.VMEM((2 * slots, width), jnp.float32),
            pltpu.VMEM((n, 2 * slots, width), jnp.float32),
            pltpu.VMEM((cuts, n, cut, group, dv), jnp.int16),
            pltpu.VMEM((cuts, n, cut, group, dv), jnp.int16),
            pltpu.VMEM((cuts, n, slots, width), jnp.float32),
            pltpu.VMEM((cuts, n, slots, width), jnp.float32),
            dma((4,)), dma((cuts, n)), dma((n,)), dma((n,)),
            dma((cuts, n)), dma((cuts, n)), dma((cuts, n)), dma((cuts, n)), dma((cuts, n)), dma((cuts, n)),
        ],
        compiler_params=pltpu.CompilerParams(
            collective_id=0, has_side_effects=True, vmem_limit_bytes=67043328),
    )(lengths, slot_request, q_latent, q_rope, cache_latent, rope_keys, value_up)
    return jnp.transpose(out.reshape(heads, toks, slots, dv), (2, 1, 0, 3))


def solution(mesh):
    in_specs = (
        P("groups", None, "head", None),
        P("groups", None, "head", None),
        P(("groups", "rep"), "seq", None),
        P(("groups", "rep"), None, "seq"),
        P(("groups", "rep")),
        P(("groups", "rep")),
        P("head", None, None),
    )
    out_specs = P(("groups", "rep"), None, "head", None)
    return jax.shard_map(
        functools.partial(per_device, mesh.shape["seq"]),
        mesh=mesh, in_specs=in_specs, out_specs=out_specs, check_vma=False,
    )
```

time: 32.2 us -> 27.7 us (0.86)
  Pallas kernels: 30.3 us -> 25.8 us
    pallas_call x1, Pallas kernels: 30.3 us -> 25.8 us  [per_device(): pl.pallas_call(functools.partial(kernel, n, cuts), out_shape=jax.ShapeDty...]
where the time goes in v2:
time: 27.7 us; the launch traced here: 27.5 us
  Pallas kernels  25.8 us (93%)
  local copies, waits for them, and re-layouts  1.72 us (6%)
    pallas_call x1, Pallas kernels, per_device(): pl.pallas_call(functools.partial(kernel, n, cuts), out_shape=jax.ShapeDty...  25.8 us
    reshape x1, local copies, waits for them, and re-layouts, per_device(): return jnp.transpose(out.reshape(heads, toks, slots, dv), (2, 1, 0, 3))  1.72 us

profile of v2, /device:TPU:0, one launch (start us, length us, event | category | flops | bytes accessed | tf_op | source)
XLA Modules:
  0.0 27.5 jit_solution(16701777922119657908)
XLA Ops:
  0.0 25.8 %shard_map.73 = bf16[64,16,128]{2,1,0:T(8,128)(2,1)} custom-call(s32[8]{0:T(128)} %lengths_ref.1, s32[8]{0:T(128)} %request_ref.1, bf16[16,2,64,512]{3,2,1,0:T(8,128)(2,1)} %qlat_hbm.1, bf16[16,2,64,64]{3,2,1,0:T(8,128)(2,1)} %qrot_hbm.1, bf16[8,128,512]{2,1,0:T(8,128)(2,1)} %cache_hbm.1, bf16[8,64,128]{2,1,0:T(8,128)(2,1)} %rope_hbm.1, ...), custom_call_target="tpu_custom_call" | custom-call | tf_op jit(solution)/shard_map/pallas_call | solution.py:192
  25.8 1.7 %copy.10 = bf16[64,2,8,128]{3,0,1,2:T(8,128)(2,1)} copy(bf16[64,2,8,128]{3,2,1,0:T(8,128)(2,1)} %bitcast.4) | data formatting | bytes 524288 | tf_op jit(solution)/shard_map/reshape | solution.py:218

commit v3 on v1

v3 whole, which is shorter than its diff:
```python
import functools

import jax
import jax.numpy as jnp
from jax import lax
from jax.experimental import pallas as pl
from jax.experimental.pallas import tpu as pltpu
from jax.sharding import PartitionSpec as P

ROPE = 64
NOPE = 128
MESH = pl.DeviceIdType.MESH
LANES = 128
CODE = 32767.0


negative_fill = -1e30


def kernel(n, lengths_ref, request_ref, qlat_hbm, qrot_hbm, cache_hbm, rope_hbm, w_hbm, out_ref,
           qlat, qrot, cache, rope, w, weights, x, own, turned, send, recv, meta_out, meta_in,
           load_sem, w_sem, rs_ssem, rs_rsem, meta_ssem, meta_rsem, ag_ssem, ag_rsem):
    slots, page, latent = cache.shape
    toks, heads = qlat.shape[1], qlat.shape[2]
    rows = toks * heads
    group = toks * slots
    per = heads // n
    direct = per % 16 == 0
    me = lax.axis_index("seq")
    order = [3, 2, 1] if n == 4 else list(range(1, n))

    def peer(k):
        if n == 4:
            return (me, me + 1 - 2 * lax.rem(me, 2), lax.rem(me + 2, 4), 3 - me)[k]
        return lax.rem(me + k, n)

    loads = [
        pltpu.make_async_copy(src, dst, load_sem.at[i])
        for i, (src, dst) in enumerate(
            ((qlat_hbm, qlat), (cache_hbm, cache), (qrot_hbm, qrot), (rope_hbm, rope)))
    ]
    for copy in loads:
        copy.start()

    def w_load(k):
        part = pl.ds(peer(k) * per, per)
        return pltpu.make_async_copy(w_hbm.at[part], w.at[part], w_sem.at[k])

    barrier = pltpu.get_barrier_semaphore()
    for k in order:
        pl.semaphore_signal(barrier, inc=1, device_id={"seq": peer(k)}, device_id_type=MESH)

    for copy in loads:
        copy.wait()
    for k in order + [0]:
        w_load(k).start()

    softmax_scale = (NOPE + ROPE) ** (-0.5)
    lane = lax.broadcasted_iota(jnp.int32, (rows, LANES), 1)
    token = lax.broadcasted_iota(jnp.int32, (rows, page), 0) // heads
    position = me * page + lax.broadcasted_iota(jnp.int32, (rows, page), 1)
    stat = jnp.zeros((rows, LANES), jnp.float32)
    for b in range(slots):
        r = request_ref[b]
        ql = qlat[r].reshape(rows, latent)
        qr = qrot[r].reshape(rows, qrot.shape[3])
        s = lax.dot_general(ql, cache[b], (((1,), (1,)), ((), ())), preferred_element_type=jnp.float32)
        s = s + jnp.dot(qr, rope[b], preferred_element_type=jnp.float32)
        s = s * softmax_scale
        visible = position < lengths_ref[b] - toks + 1 + token
        masked = jnp.where(visible, s, negative_fill)
        top = jnp.max(masked, axis=1, keepdims=True)
        e = jnp.where(visible, jnp.exp(masked - top), 0.0)
        den = jnp.sum(e, axis=1, keepdims=True)
        stat = jnp.where(lane == b, top, stat)
        stat = jnp.where(lane == slots + b, den, stat)
        weights[b] = e.astype(jnp.bfloat16)
    width = meta_out.shape[3]
    if rows < width:
        stat = jnp.concatenate([stat, jnp.zeros((width - rows, LANES), jnp.float32)], axis=0)
    mine = jnp.transpose(stat)[: 2 * slots]
    meta_lane = lax.broadcasted_iota(jnp.int32, (2 * slots, width), 1)
    scale_lane = meta_lane[:slots]

    def stats_of(dest):
        picked = mine
        for t in range(toks):
            shift = lax.rem(2 * width - t * (heads - per) - dest * per, width)
            moved = pltpu.roll(mine, shift, 1)
            picked = moved if t == 0 else jnp.where(meta_lane >= t * per, moved, picked)
        return picked[:slots], picked[slots:]

    def remote(src, dst, ssem, rsem, k):
        return pltpu.make_async_remote_copy(
            src_ref=src, dst_ref=dst, send_sem=ssem, recv_sem=rsem,
            device_id={"seq": peer(k)}, device_id_type=MESH)

    def rs_copy(k):
        return remote(send.at[k], recv.at[k], rs_ssem.at[k], rs_rsem.at[k], k)

    def meta_copy(k):
        return remote(meta_out.at[k], meta_in.at[k], meta_ssem.at[k], meta_rsem.at[k], k)

    def ag_copy(k):
        part = pl.ds(me * per, per)
        part = out_ref.at[:, part] if direct else out_ref.at[part]
        return remote(part, part, ag_ssem.at[k], ag_rsem.at[k], k)

    for b in range(slots):
        po = jnp.dot(weights[b], cache[b], preferred_element_type=jnp.float32)
        for t in range(toks):
            for i in range(latent // LANES):
                x[i, pl.ds(t * slots + b, heads, stride=group), :] = (
                    po[t * heads:(t + 1) * heads, i * LANES:(i + 1) * LANES])

    for k in order + [0]:
        w_load(k).wait()
        scale = jnp.zeros((slots, width), jnp.float32)
        for j in range(per):
            h = peer(k) * per + j
            base = pl.multiple_of(h * group, group)
            xs = jnp.concatenate([x[i, pl.ds(base, group), :] for i in range(latent // LANES)], axis=1)
            hi = xs.astype(jnp.bfloat16)
            lo = (xs - hi.astype(jnp.float32)).astype(jnp.bfloat16)
            both = jnp.dot(jnp.concatenate([hi, lo], axis=0), w[h], preferred_element_type=jnp.float32)
            part = both[:group] + both[group:]
            if k == 0:
                own[j] = part
            else:
                peak = jnp.maximum(jnp.max(jnp.abs(part), axis=1, keepdims=True), 1e-30)
                send[k, j] = jnp.round(part * (CODE / peak)).astype(jnp.int32).astype(jnp.int16)
                for t in range(toks):
                    scale = jnp.where(scale_lane == t * per + j, peak[t * slots:(t + 1) * slots], scale)
        if k != 0:
            top, den = stats_of(peer(k))
            meta_out[k, 0] = scale * (1.0 / CODE)
            meta_out[k, 1] = top
            meta_out[k, 2] = den
            if k == order[0]:
                pl.semaphore_wait(barrier, n - 1)
            meta_copy(k).start()
            rs_copy(k).start()

    tops, dens, scales = [], [], [None]
    top, den = stats_of(me)
    tops.append(top)
    dens.append(den)
    for k in range(1, n):
        meta_copy(k).wait_recv()
        scales.append(meta_in[k, 0])
        tops.append(meta_in[k, 1])
        dens.append(meta_in[k, 2])
    largest = functools.reduce(jnp.maximum, tops)
    factors = [jnp.exp(t - largest) for t in tops]
    total = functools.reduce(lambda a, b: a + b, [f * d for f, d in zip(factors, dens)])
    coefs = []
    for k in range(n):
        ratio = factors[k] / total
        if k:
            ratio = ratio * scales[k]
        coefs.append(jnp.concatenate(
            [pltpu.roll(ratio, width - t * per, 1) if t else ratio for t in range(toks)], axis=0))
    for k in order:
        rs_copy(k).wait_recv()
    for j in range(per):
        acc = own[j] * coefs[0][:, j:j + 1]
        for k in range(1, n):
            acc = acc + recv[k, j].astype(jnp.float32) * coefs[k][:, j:j + 1]
        if direct:
            turned[pl.ds(j, group, stride=per), :] = acc
        else:
            out_ref[me * per + j] = acc.astype(jnp.bfloat16)
    if direct:
        place = pl.multiple_of(me * per, per)
        for t in range(toks):
            for b in range(slots):
                row = (t * slots + b) * per
                out_ref[b * toks + t, pl.ds(place, per), :] = turned[row:row + per, :].astype(jnp.bfloat16)
    for k in order:
        ag_copy(k).start()
    for k in order:
        meta_copy(k).wait_send()
        rs_copy(k).wait_send()
    for k in order:
        ag_copy(k).wait()


def per_device(n, q_latent, q_rope, cache_latent, rope_keys, lengths, slot_request, value_up):
    toks, heads = q_latent.shape[1], q_latent.shape[2]
    slots, page, latent = cache_latent.shape
    dv = value_up.shape[2]
    group = toks * slots
    per = heads // n
    direct = per % 16 == 0
    rows = toks * heads
    width = -(-rows // LANES) * LANES
    hbm = pl.BlockSpec(memory_space=pltpu.HBM)
    smem = pl.BlockSpec(memory_space=pltpu.SMEM)
    dma = pltpu.SemaphoreType.DMA
    out = pl.pallas_call(
        functools.partial(kernel, n),
        out_shape=jax.ShapeDtypeStruct(
            (group, heads, dv) if direct else (heads, group, dv), jnp.bfloat16),
        in_specs=[smem, smem, hbm, hbm, hbm, hbm, hbm],
        out_specs=pl.BlockSpec(memory_space=pltpu.VMEM),
        scratch_shapes=[
            pltpu.VMEM(q_latent.shape, jnp.bfloat16),
            pltpu.VMEM(q_rope.shape, jnp.bfloat16),
            pltpu.VMEM(cache_latent.shape, jnp.bfloat16),
            pltpu.VMEM(rope_keys.shape, jnp.bfloat16),
            pltpu.VMEM(value_up.shape, jnp.bfloat16),
            pltpu.VMEM((slots, rows, page), jnp.bfloat16),
            pltpu.VMEM((latent // LANES, heads * group, LANES), jnp.float32),
            pltpu.VMEM((per, group, dv), jnp.float32),
            pltpu.VMEM((per * group, dv), jnp.float32),
            pltpu.VMEM((n, per, group, dv), jnp.int16),
            pltpu.VMEM((n, per, group, dv), jnp.int16),
            pltpu.VMEM((n, 3, slots, width), jnp.float32),
            pltpu.VMEM((n, 3, slots, width), jnp.float32),
            dma((4,)), dma((n,)), dma((n,)), dma((n,)), dma((n,)), dma((n,)), dma((n,)), dma((n,)),
        ],
        compiler_params=pltpu.CompilerParams(
            collective_id=0, has_side_effects=True, vmem_limit_bytes=67043328),
    )(lengths, slot_request, q_latent, q_rope, cache_latent, rope_keys, value_up)
    if direct:
        return out.reshape(slots, toks, heads, dv)
    return jnp.transpose(out.reshape(heads, toks, slots, dv), (2, 1, 0, 3))


def solution(mesh):
    in_specs = (
        P("groups", None, "head", None),
        P("groups", None, "head", None),
        P(("groups", "rep"), "seq", None),
        P(("groups", "rep"), None, "seq"),
        P(("groups", "rep")),
        P(("groups", "rep")),
        P("head", None, None),
    )
    out_specs = P(("groups", "rep"), None, "head", None)
    return jax.shard_map(
        functools.partial(per_device, mesh.shape["seq"]),
        mesh=mesh, in_specs=in_specs, out_specs=out_specs, check_vma=False,
    )
```

time: 32.2 us -> 25.2 us (0.78)
  Pallas kernels: 30.3 us -> 23.4 us
    pallas_call x1, Pallas kernels: 30.3 us -> 23.4 us  [per_device(): pl.pallas_call(functools.partial(kernel, n), out_shape=jax.ShapeDtypeStru...]
    reshape x1 -> x0, local copies, waits for them, and re-layouts: 1.72 us -> none  [per_device(): return jnp.transpose(out.reshape(heads, toks, slots, dv), (2, 1, 0, 3))]
    unnamed x0 -> x1, local copies, waits for them, and re-layouts: none -> 1.67 us
where the time goes in v3:
time: 25.2 us; the launch traced here: 25.1 us
  Pallas kernels  23.4 us (93%)
  local copies, waits for them, and re-layouts  1.67 us (7%)
    pallas_call x1, Pallas kernels, per_device(): pl.pallas_call(functools.partial(kernel, n), out_shape=jax.ShapeDtypeStru...  23.4 us
    unnamed x1, local copies, waits for them, and re-layouts  1.67 us

profile of v3, /device:TPU:0, one launch (start us, length us, event | category | flops | bytes accessed | tf_op | source)
XLA Modules:
  0.0 25.1 jit_solution(14343730361224669629)
XLA Ops:
  0.0 23.4 %shard_map.73 = bf16[16,64,128]{2,1,0:T(8,128)(2,1)} custom-call(s32[8]{0:T(128)} %lengths_ref.1, s32[8]{0:T(128)} %request_ref.1, bf16[16,2,64,512]{3,2,1,0:T(8,128)(2,1)} %qlat_hbm.1, bf16[16,2,64,64]{3,2,1,0:T(8,128)(2,1)} %qrot_hbm.1, bf16[8,128,512]{2,1,0:T(8,128)(2,1)} %cache_hbm.1, bf16[8,64,128]{2,1,0:T(8,128)(2,1)} %rope_hbm.1, ...), custom_call_target="tpu_custom_call" | custom-call | tf_op jit(solution)/shard_map/pallas_call | solution.py:200
  23.4 1.7 %copy.9 = bf16[8,2,64,128]{3,2,1,0:T(8,128)(2,1)} copy(bf16[8,2,64,128]{3,2,1,0:T(8,128)(2,1)} %bitcast.1) | data formatting | bytes 524288

commit v4 on v3

--- a/solution.py
+++ b/solution.py
@@ -27,11 +27,9 @@
     per = heads // n
     direct = per % 16 == 0
     me = lax.axis_index("seq")
-    order = [3, 2, 1] if n == 4 else list(range(1, n))
+    order = sorted(range(1, n), key=lambda k: abs(k - n / 2))
 
     def peer(k):
-        if n == 4:
-            return (me, me + 1 - 2 * lax.rem(me, 2), lax.rem(me + 2, 4), 3 - me)[k]
         return lax.rem(me + k, n)
 
     loads = [

time: 25.2 us -> 24.6 us (0.976)
  Pallas kernels: 23.4 us -> 22.7 us
    pallas_call x1, Pallas kernels: 23.4 us -> 22.7 us  [per_device(): pl.pallas_call(functools.partial(kernel, n), out_shape=jax.ShapeDtypeStru...]
where the time goes in v4:
time: 24.6 us; the launch traced here: 24.4 us
  Pallas kernels  22.7 us (92%)
  local copies, waits for them, and re-layouts  1.67 us (7%)
    pallas_call x1, Pallas kernels, per_device(): pl.pallas_call(functools.partial(kernel, n), out_shape=jax.ShapeDtypeStru...  22.7 us
    unnamed x1, local copies, waits for them, and re-layouts  1.67 us

profile of v4, /device:TPU:0, one launch (start us, length us, event | category | flops | bytes accessed | tf_op | source)
XLA Modules:
  0.0 24.4 jit_solution(9127250885037923660)
XLA Ops:
  0.0 22.7 %shard_map.73 = bf16[16,64,128]{2,1,0:T(8,128)(2,1)} custom-call(s32[8]{0:T(128)} %lengths_ref.1, s32[8]{0:T(128)} %request_ref.1, bf16[16,2,64,512]{3,2,1,0:T(8,128)(2,1)} %qlat_hbm.1, bf16[16,2,64,64]{3,2,1,0:T(8,128)(2,1)} %qrot_hbm.1, bf16[8,128,512]{2,1,0:T(8,128)(2,1)} %cache_hbm.1, bf16[8,64,128]{2,1,0:T(8,128)(2,1)} %rope_hbm.1, ...), custom_call_target="tpu_custom_call" | custom-call | tf_op jit(solution)/shard_map/pallas_call | solution.py:198
  22.7 1.7 %copy.9 = bf16[8,2,64,128]{3,2,1,0:T(8,128)(2,1)} copy(bf16[8,2,64,128]{3,2,1,0:T(8,128)(2,1)} %bitcast.1) | data formatting | bytes 524288
